TPU v7x, 32 devices: a whole 2x2x4 slice. The times are simulated.
32 devices in a mesh: tab: 8 (over y, x, core), rep: 4 (over z).
Axes of the slice: x: 2, y: 2, z: 4, core: 2. Of those that a mesh axis runs over, the one named last changes fastest.
Arguments:
- pooled: bfloat16 [64, 4096, 128], P('tab', 'rep'), may hold values from -6 to 6
- widths: int32 [64], replicated, may hold values from 16 to 128, as said below
- placement: int32 [64], replicated, may hold values from 0 to 63, each once
- route: int32 [4, 1024], P('rep'), may hold values from 0 to 1023, each once within a row
- labels: int32 [4, 1024], P('rep'), may hold values 0 or 1
- proj: bfloat16 [64, 128, 32], replicated, may hold values from -0.5 to 0.5
- senet_in: float32 [64, 32], replicated, may hold values from -6 to 6
- senet_out: float32 [32, 64], replicated, may hold values from -1 to 1
- bilinear: float32 [32, 32], replicated, may hold values from -1 to 1
- w_first: bfloat16 [4096, 256], replicated, may hold values from -0.09375 to 0.09375
- w_second: bfloat16 [256, 256], replicated, may hold values from -0.75 to 0.75
- w_last: bfloat16 [256], replicated, may hold values from -0.375 to 0.375
Outputs:
- scores: float32 [4, 1024], P('rep', 'tab')
- d_pooled: bfloat16 [64, 4096, 128], P('tab', 'rep')
- d_proj: float32 [64, 128, 32], P('tab')
- d_senet_in: float32 [64, 32], replicated
- d_senet_out: float32 [32, 64], replicated
- d_bilinear: float32 [32, 32], replicated
- d_first: float32 [4096, 256], P('tab')
- d_second: float32 [256, 256], replicated
- d_last: float32 [256], replicated
Inputs may be any that keep to these rules, and one draw needn't show every extreme that they name: `widths`: each field's width is 128, 64, 32 or 16. `placement`: a permutation of the fields. `route`: each row is a permutation of 0 to 1023.
All inputs are finite; a program needn't handle non-finite values. No bound on the sum of `labels` on one device may be relied on, other than what follows from the above.
Results may differ from a plain program's by a relative error of at most 0.017.
Values may be sent and summed in bfloat16 or wider, within the bound.
No kernel may reach another device: no remote copies, remote signals or barrier semaphores. Data moves between devices by JAX's collectives and lax.ppermute only.
A program may use at most 64 MiB of HBM per device.

v0:
```python
import functools

import jax
import jax.numpy as jnp
from jax import lax
from jax.experimental import pallas as pl
from jax.experimental.pallas import tpu as pltpu
from jax.sharding import PartitionSpec as P


PRECISE = lax.Precision.HIGHEST
BF = jnp.bfloat16
F32 = jnp.float32
VMEM = pltpu.VMEM
NN = (((1,), (0,)), ((), ()))
NT = (((1,), (1,)), ((), ()))
TN = (((0,), (0,)), ((), ()))


def dot(a, b, dims=NN, precision=None):
    return lax.dot_general(a, b, dims, precision=precision, preferred_element_type=F32)


def split(x):
    high = x.astype(BF)
    return high, (x - high.astype(F32)).astype(BF)


def silu_slope(pre_act):
    logistic = jax.nn.sigmoid(pre_act)
    return logistic * (1.0 + pre_act * (1.0 - logistic))


def vspec():
    return pl.BlockSpec(memory_space=VMEM)


def hspec():
    return pl.BlockSpec(memory_space=pltpu.HBM)


def far(*arrays):
    return tuple(pltpu.with_memory_space_constraint(a, pltpu.HBM) for a in arrays)


def params(mebibytes):
    return pltpu.CompilerParams(vmem_limit_bytes=mebibytes << 20)


def embed_body(widths_hbm, placement_hbm, pooled, proj, *refs):
    weight_out, *outs = refs[:-8]
    widths, placement, rows_in, gathered, weights, staged, sems, out_sems = refs[-8:]
    slots, _, padded = rows_in.shape
    width = proj.shape[1]
    tab, _, owner = staged.shape
    mine = lax.axis_index("tab")
    first = mine * slots
    tables = [
        pltpu.make_async_copy(placement_hbm, placement, sems.at[slots]),
        pltpu.make_async_copy(widths_hbm, widths, sems.at[slots + 1]),
    ]
    for copy in tables:
        copy.start()
    whole = pltpu.make_async_copy(proj, gathered, sems.at[slots + 2])
    whole.start()
    large = [pltpu.make_async_copy(pooled.at[s], rows_in.at[s], sems.at[s]) for s in range(slots)]
    for copy in large:
        copy.start()
    for copy in tables:
        copy.wait()
    whole.wait()
    lane = lax.broadcasted_iota(jnp.int32, (width, padded), 1)
    gone = []
    for s in range(slots):
        part = slice(s * width, (s + 1) * width)
        field = placement[first + s]
        weight = jnp.where(lane < widths[field], gathered[field].astype(F32), 0.0).astype(BF)
        weights[part, :] = weight
        large[s].wait()
        embeds = dot(weight, rows_in[s], NT).astype(BF)
        for o in range(tab):
            staged[o, part, :] = embeds[:, o * owner : (o + 1) * owner]
    pairs = [(staged.at[mine ^ q], outs[q]) for q in range(1, tab)] + [(staged.at[mine], outs[0]), (weights, weight_out)]
    for i, (source, target) in enumerate(pairs):
        copy = pltpu.make_async_copy(source, target, out_sems.at[i])
        copy.start()
        gone.append(copy)
    for copy in gone:
        copy.wait()


def embed_slots(widths, placement, pooled, proj, tab):
    slots, rows, padded = pooled.shape
    width = proj.shape[1]
    fields = placement.shape[0]
    return pl.pallas_call(
        embed_body,
        out_shape=(pltpu.HBM((slots * width, padded), BF),) + (pltpu.HBM((slots * width, rows // tab), BF),) * tab,
        in_specs=[hspec()] * 4,
        out_specs=(hspec(),) * (1 + tab),
        scratch_shapes=[
            pltpu.SMEM((fields,), jnp.int32),
            pltpu.SMEM((fields,), jnp.int32),
            pltpu.VMEM((slots, rows, padded), BF),
            pltpu.VMEM(proj.shape, BF),
            pltpu.VMEM((slots * width, padded), BF),
            pltpu.VMEM((tab, slots * width, rows // tab), BF),
            pltpu.SemaphoreType.DMA((slots + 3,)),
            pltpu.SemaphoreType.DMA((tab + 1,)),
        ],
        compiler_params=params(12),
        name="embed_slots",
    )(*far(widths, placement, pooled, proj))


def prepare_body(order, first_hbm, second_hbm, bilinear_hbm, last_hbm, *rest):
    outs, (first, second, bilinear, last), made, sems, out_sems = rest[:6], rest[6:10], rest[10:16], rest[16], rest[17]
    first_turned, second_turned, kron_high, kron_low, back_high, last_column = made
    copies = [
        pltpu.make_async_copy(source, target, sems.at[i])
        for i, (source, target) in enumerate(
            ((bilinear_hbm, bilinear), (last_hbm, last), (second_hbm, second), (first_hbm, first))
        )
    ]
    for copy in copies:
        copy.start()
    leaving = [pltpu.make_async_copy(made[i], outs[i], out_sems.at[i]) for i in range(len(outs))]
    width = bilinear.shape[0]
    side = kron_high.shape[0]
    copies[0].wait()
    tiled = jnp.concatenate([bilinear[...]] * (side // width), axis=1)
    tiled = jnp.concatenate([tiled] * (side // width), axis=0)
    row = lax.broadcasted_iota(jnp.int32, (side, side), 0) // width
    column = lax.broadcasted_iota(jnp.int32, (side, side), 1) // width
    kron = jnp.where(row == column, tiled, 0.0)
    back_high[...] = kron.astype(BF)
    kron_high[...], kron_low[...] = split(kron.T)
    hidden = last.shape[1]
    row = lax.broadcasted_iota(jnp.int32, (hidden, hidden), 0)
    column = lax.broadcasted_iota(jnp.int32, (hidden, hidden), 1)
    copies[1].wait()
    last_column[...] = jnp.sum(jnp.where(row == column, last[...].astype(F32), 0.0), axis=1, keepdims=True)
    copies[2].wait()
    second_turned[...] = second[...].T
    for copy in leaving[1:]:
        copy.start()
    copies[3].wait()
    step = min(512, first.shape[0])
    for g in range(0, first.shape[0], step):
        first_turned[:, g : g + step] = first[g : g + step, :].T
    leaving[0].start()
    for copy in leaving:
        copy.wait()


def prepare(order, w_first, w_second, bilinear, w_last):
    total, hidden = w_first.shape
    side = min(256, total)
    shapes = (
        ((hidden, total), BF), ((hidden, hidden), BF), ((side, side), BF), ((side, side), BF), ((side, side), BF),
        ((hidden, 1), F32),
    )
    return pl.pallas_call(
        prepare_body,
        out_shape=tuple(pltpu.HBM(s, d) for s, d in shapes),
        in_specs=[hspec()] * 5,
        out_specs=tuple(hspec() for _ in shapes),
        scratch_shapes=[
            pltpu.VMEM(w_first.shape, BF),
            pltpu.VMEM(w_second.shape, BF),
            pltpu.VMEM(bilinear.shape, F32),
            pltpu.VMEM(w_last.shape, BF),
            *[pltpu.VMEM(s, d) for s, d in shapes],
            pltpu.SemaphoreType.DMA((4,)),
            pltpu.SemaphoreType.DMA((len(shapes),)),
        ],
        compiler_params=params(12),
        name="prepare",
    )(*far(order, w_first, w_second, bilinear, w_last))


def owner_body(placement_hbm, *refs):
    *refs, joined, send, embeds_ref, product_ref, grad_ref, gate_ref, flat, sems, out_sems = refs
    count = 11
    loaded = refs[-count:]
    placement, arrived = refs[-count - 2 : -count]
    kept_out, moved_out, send_hbm = refs[-count - 5 : -count - 2]
    sources = refs[: -count - 5]
    tab = arrived.shape[0]
    labels, senet_in, senet_out, kron_high, kron_low, first_turned, second_turned, last, second, back_high, first = loaded
    tables = pltpu.make_async_copy(placement_hbm, placement, sems.at[count])
    tables.start()
    pieces = [pltpu.make_async_copy(sources[q], arrived.at[q], sems.at[count + 1 + q]) for q in range(tab)]
    for copy in pieces:
        copy.start()
    loads = [pltpu.make_async_copy(sources[tab + i], loaded[i], sems.at[i]) for i in range(count)]
    for copy in loads[:6]:
        copy.start()

    fields = placement.shape[0]
    lanes = arrived.shape[2]
    total = tab * arrived.shape[1]
    width = total // fields
    factor = fields ** -0.5
    chunk = kron_high.shape[0]
    per = chunk // width
    hidden = second.shape[0]
    depth = send.shape[1]
    slots = fields // tab
    rows = 2 * total // tab
    step = min(chunk, rows)
    mine = lax.axis_index("tab")
    core = mine % 2
    tables.wait()
    for q in range(tab):
        pieces[q].wait()
        for i in range(slots):
            spot = pl.multiple_of(placement[(mine ^ q) * slots + i] * width, width)
            embeds_ref[pl.ds(spot, width), :] = arrived[q, i * width : (i + 1) * width, :]

    dense3 = embeds_ref[...].astype(F32).reshape(fields, width, lanes)
    squeeze = jnp.sum(dense3, axis=1) * (1.0 / width)
    for copy in loads[:5]:
        copy.wait()
    for copy in loads[6:]:
        copy.start()
    pre_one = dot(senet_in[...], squeeze, NN, PRECISE)
    act_one = pre_one * jax.nn.sigmoid(pre_one)
    weights = jax.nn.sigmoid(dot(senet_out[...], act_one, TN, PRECISE))
    sum_plain = jnp.zeros((width, lanes), F32)
    sum_scaled = jnp.zeros((width, lanes), F32)
    for f in range(fields):
        one = embeds_ref[f * width : (f + 1) * width, :].astype(F32)
        sum_plain = sum_plain + one
        sum_scaled = sum_scaled + one * weights[f : f + 1, :]
    for g in range(0, total, chunk):
        block = embeds_ref[g : g + chunk, :]
        product = dot(kron_high[...], block) + dot(kron_low[...], block)
        product_ref[g : g + chunk, :] = product
        product3 = product.reshape(per, width, lanes) * factor
        dense = block.astype(F32).reshape(per, width, lanes)
        scale = weights[g // width : g // width + per][:, None, :]
        plain = (product3 * (sum_plain[None] - dense)).reshape(chunk, lanes).astype(BF)
        scaled = (product3 * scale * (sum_scaled[None] - dense * scale)).reshape(chunk, lanes).astype(BF)
        for start, values in ((g, plain), (total + g, scaled)):
            for piece in range(0, chunk, step):
                owner, spot = divmod(start + piece, rows)
                at = owner // 2 * rows + spot
                joined[(owner % 2) ^ core, at : at + step, :] = values[piece : piece + step]
    blocks = [joined[(o % 2) ^ core, o // 2 * rows : (o // 2 + 1) * rows, :] for o in range(tab)]
    loads[5].wait()
    pre_hidden = dot(first_turned[...], jnp.concatenate(blocks, axis=0))
    for copy in loads[6:]:
        copy.wait()
    hidden_one = (pre_hidden * jax.nn.sigmoid(pre_hidden)).astype(BF)
    pre_second = dot(second_turned[...], hidden_one)
    hidden_two = (pre_second * jax.nn.sigmoid(pre_second)).astype(BF)
    hidden_wide = hidden_two.astype(F32)
    last_wide = last[...]
    logits = jnp.sum(last_wide * hidden_wide, axis=0, keepdims=True)
    grad_logit = jax.nn.sigmoid(logits) - labels[pl.ds(mine, 1), :].astype(F32)
    d_last = jnp.sum(hidden_wide * grad_logit, axis=1, keepdims=True)
    d_pre_two = (grad_logit * last_wide * silu_slope(pre_second)).astype(BF)
    flat[:hidden, :] = dot(hidden_one, d_pre_two, NT)
    d_pre_one = (dot(second[...], d_pre_two) * silu_slope(pre_hidden)).astype(BF)
    joined[0, total:, :] = d_pre_one
    joined[1, total:, :] = d_pre_one
    leave_moved = pltpu.make_async_copy(joined.at[1], moved_out, out_sems.at[1])
    leave_moved.start()
    leave_kept = pltpu.make_async_copy(joined.at[0], kept_out, out_sems.at[0])
    leave_kept.start()

    rest_plain = jnp.zeros((width, lanes), F32)
    rest_scaled = jnp.zeros((width, lanes), F32)
    bil = jnp.zeros((chunk, chunk), F32)
    d_weight_parts = []
    for g in range(0, total, chunk):
        d_plain = dot(first[g : g + chunk, :], d_pre_one).reshape(per, width, lanes)
        d_scaled = dot(first[total + g : total + g + chunk, :], d_pre_one).reshape(per, width, lanes)
        block = embeds_ref[g : g + chunk, :]
        dense = block.astype(F32).reshape(per, width, lanes)
        scale = weights[g // width : g // width + per][:, None, :]
        product = product_ref[g : g + chunk, :].reshape(per, width, lanes) * factor
        others_scaled = d_scaled * product
        d_others_plain = d_plain * product
        d_others_scaled = others_scaled * scale
        rest_plain = rest_plain + jnp.sum(d_others_plain, axis=0)
        rest_scaled = rest_scaled + jnp.sum(d_others_scaled, axis=0)
        away_scaled = sum_scaled[None] - dense * scale
        d_product = (d_plain * (sum_plain[None] - dense) + d_scaled * scale * away_scaled) * factor
        direct = d_product.reshape(chunk, lanes).astype(BF)
        bil = bil + dot(block, direct, NT)
        back = dot(back_high[...], direct).reshape(per, width, lanes)
        grad = back - d_others_plain - d_others_scaled * scale
        grad_ref[g : g + chunk, :] = grad.reshape(chunk, lanes)
        d_weight_parts.append(jnp.sum(others_scaled * away_scaled - dense * d_others_scaled, axis=1))
    d_bil = bil[0:width, 0:width]
    for i in range(1, per):
        d_bil = d_bil + bil[i * width : (i + 1) * width, i * width : (i + 1) * width]
    dense3 = embeds_ref[...].astype(F32).reshape(fields, width, lanes)
    d_weights = jnp.concatenate(d_weight_parts, axis=0) + jnp.sum(dense3 * rest_scaled[None], axis=1)
    d_pre_w = d_weights * weights * (1.0 - weights)
    d_out = dot(act_one, d_pre_w, NT, PRECISE)
    d_act = dot(senet_out[...], d_pre_w, NN, PRECISE) * silu_slope(pre_one)
    d_in = dot(d_act, squeeze, NT, PRECISE)
    d_squeeze = dot(senet_in[...], d_act, TN, PRECISE) * (1.0 / width)
    gate_ref[0] = weights
    gate_ref[1] = d_squeeze
    for s in range(fields):
        spot = pl.multiple_of(placement[s] * width, width)
        at = s % slots * width
        grad = grad_ref[pl.ds(spot, width), :] + rest_plain
        grad = grad + (gate_ref[0, pl.ds(placement[s], 1), :] * rest_scaled + gate_ref[1, pl.ds(placement[s], 1), :])
        send[s // slots, at : at + width, :] = grad.astype(BF)
    senet = senet_in.shape[0]
    lines = flat.shape[0] // tab
    columns = [d_in, d_out, d_bil] + [d_last[i : i + senet, :] for i in range(0, hidden, senet)]
    used = sum(c.shape[1] for c in columns)
    flat[hidden:, :] = jnp.zeros((flat.shape[0] - hidden, hidden), F32)
    flat[hidden : hidden + senet, :] = jnp.concatenate(columns + [jnp.zeros((senet, hidden - used), F32)], axis=1)
    high = logits.astype(BF).astype(F32)
    base = slots * width
    spare = jnp.zeros((depth - base - hidden // lanes * lines - 2, lanes), F32)
    for t in range(tab):
        band = flat[t * lines : (t + 1) * lines, :]
        pieces = [band[:, i : i + lanes] for i in range(0, hidden, lanes)] + [high, logits - high, spare]
        send[t, base:, :] = jnp.concatenate(pieces, axis=0).astype(BF)
    leave_send = pltpu.make_async_copy(send, send_hbm, out_sems.at[2])
    leave_send.start()
    leave_kept.wait()
    leave_moved.wait()
    leave_send.wait()


def depth_of(base, lines, hidden, lanes):
    return -(-(base + hidden // lanes * lines + 2) // 16) * 16


def owner_pass(placement, arrived, labels, senet_in, senet_out, kron_high, kron_low, first_turned, second_turned, last, w_second, back_high, w_first):
    tab = len(arrived)
    total, lanes = tab * arrived[0].shape[0], arrived[0].shape[1]
    senet, fields = senet_in.shape
    hidden = w_second.shape[0]
    lines = -(-(hidden + senet) // tab)
    depth = depth_of(total // tab, lines, hidden, lanes)
    pair = jax.ShapeDtypeStruct((total + hidden, lanes), BF)
    operands = (labels, senet_in, senet_out, kron_high, kron_low, first_turned, second_turned, last, w_second, back_high, w_first)
    return pl.pallas_call(
        owner_body,
        out_shape=(pair, pair, pltpu.HBM((tab, depth, lanes), BF)),
        in_specs=[hspec()] * (1 + tab + len(operands)),
        out_specs=(vspec(), vspec(), hspec()),
        scratch_shapes=[
            pltpu.SMEM((fields,), jnp.int32),
            pltpu.VMEM((tab, total // tab, lanes), BF),
            *[pltpu.VMEM(o.shape, o.dtype) for o in operands],
            pltpu.VMEM((2, total + hidden, lanes), BF),
            pltpu.VMEM((tab, depth, lanes), BF),
            pltpu.VMEM((total, lanes), BF),
            pltpu.VMEM((total, lanes), F32),
            pltpu.VMEM((total, lanes), F32),
            pltpu.VMEM((2, fields, lanes), F32),
            pltpu.VMEM((lines * tab, hidden), F32),
            pltpu.SemaphoreType.DMA((len(operands) + 1 + tab,)),
            pltpu.SemaphoreType.DMA((3,)),
        ],
        compiler_params=params(24),
        name="owner_pass",
    )(*far(placement), *arrived, *far(*operands))


def first_body(kept, came, *outs):
    chips = len(outs)
    rows, _ = outs[0].shape
    chip = lax.axis_index("tab") // 2
    right = jnp.concatenate([kept[chips * rows :, :], came[chips * rows :, :]], axis=1)
    for q in range(chips):
        part = pl.ds(pl.multiple_of((chip ^ q) * rows, rows), rows)
        left = jnp.concatenate([kept[part, :], came[part, :]], axis=1)
        outs[q][...] = dot(left, right, NT).astype(BF)


def first_grad(kept, came, chips, hidden):
    rows = (kept.shape[0] - hidden) // chips
    return pl.pallas_call(
        first_body,
        out_shape=tuple(jax.ShapeDtypeStruct((rows, hidden), BF) for _ in range(chips)),
        in_specs=[vspec()] * 2,
        out_specs=tuple(vspec() for _ in range(chips)),
        compiler_params=params(8),
        name="first_grad",
    )(kept, came)


def proj_body(
    widths_hbm, placement_hbm, pooled, grads, route_hbm, summed_out, scores,
    widths, placement, rows_in, route, sems, in_sems, *, line,
):
    slots, _, padded = rows_in.shape
    tab, _, owner = grads.shape
    mine = lax.axis_index("tab")
    first = mine * slots
    pairs = ((placement_hbm, placement), (widths_hbm, widths), (route_hbm, route))
    copies = [pltpu.make_async_copy(source, target, sems.at[i]) for i, (source, target) in enumerate(pairs)]
    large = [pltpu.make_async_copy(pooled.at[s], rows_in.at[s], in_sems.at[s]) for s in range(slots)]
    for copy in copies + large:
        copy.start()
    total = line[0]
    width = total // slots
    small = grads[0, total:, :].astype(F32)
    for o in range(1, tab):
        small = small + grads[o, total:, :].astype(F32)
    summed_out[total:, :] = small.astype(BF)
    for copy in copies:
        copy.wait()
    wanted = route[pl.ds(mine, 1), :]
    spot = lax.broadcasted_iota(jnp.int32, (owner, owner), 0)
    found = jnp.zeros((2, owner), F32)
    for o in range(tab):
        found = found + dot(grads[o, line[1] : line[1] + 2, :], (spot + o * owner == wanted).astype(F32).astype(BF))
    scores[...] = found[0:1] + found[1:2]
    lane = lax.broadcasted_iota(jnp.int32, (width, padded), 1)
    for s in range(slots):
        left = jnp.concatenate([grads[o, s * width : (s + 1) * width, :] for o in range(tab)], axis=1)
        keep = lane < widths[placement[first + s]]
        large[s].wait()
        summed_out[s * width : (s + 1) * width, :] = jnp.where(keep, dot(left, rows_in[s]), 0.0).astype(BF)


def proj_grad(widths, placement, pooled, grads, route, total, line):
    slots, _, padded = pooled.shape
    fields = placement.shape[0]
    _, depth, owner = grads.shape
    return pl.pallas_call(
        functools.partial(proj_body, line=(total, line)),
        out_shape=(jax.ShapeDtypeStruct((depth, padded), BF), jax.ShapeDtypeStruct((1, owner), F32)),
        in_specs=[hspec(), hspec(), hspec(), vspec(), hspec()],
        out_specs=(vspec(), vspec()),
        scratch_shapes=[
            pltpu.SMEM((fields,), jnp.int32),
            pltpu.SMEM((fields,), jnp.int32),
            pltpu.VMEM(pooled.shape, BF),
            pltpu.VMEM(route.shape, jnp.int32),
            pltpu.SemaphoreType.DMA((3,)),
            pltpu.SemaphoreType.DMA((slots,)),
        ],
        compiler_params=params(8),
        name="proj_grad",
    )(*far(widths, placement, pooled), grads, *far(route))


def pooled_body(weight_hbm, grads_any, d_pooled, weight, grads, made, spread, sems, out_sems):
    slots, _, padded = made.shape
    tab, total, owner = grads.shape
    width = total // slots
    copies = [
        pltpu.make_async_copy(weight_hbm, weight, sems.at[0]),
        pltpu.make_async_copy(grads_any.at[:, pl.ds(0, total), :], grads, sems.at[1]),
    ]
    for copy in copies:
        copy.start()
    spread[...] = jnp.zeros(spread.shape, BF)
    copies[0].wait()
    for s in range(slots):
        spread[s * width : (s + 1) * width, s * padded : (s + 1) * padded] = weight[s * width : (s + 1) * width, :]
    copies[1].wait()
    gone = []
    for o in range(tab):
        part = slice(o * owner, (o + 1) * owner)
        back = dot(grads[o], spread[...], TN).astype(BF)
        for s in range(slots):
            made[s, part, :] = back[:, s * padded : (s + 1) * padded]
        copy = pltpu.make_async_copy(made.at[:, part, :], d_pooled.at[:, part, :], out_sems.at[o])
        copy.start()
        gone.append(copy)
    for copy in gone:
        copy.wait()


def pooled_grad(pooled, weight, grads):
    slots, _, padded = pooled.shape
    total = weight.shape[0]
    tab, _, owner = grads.shape
    return pl.pallas_call(
        pooled_body,
        out_shape=pltpu.HBM(pooled.shape, BF),
        in_specs=[hspec()] * 2,
        out_specs=hspec(),
        scratch_shapes=[
            pltpu.VMEM(weight.shape, BF),
            pltpu.VMEM((tab, total, owner), BF),
            pltpu.VMEM(pooled.shape, BF),
            pltpu.VMEM((total, slots * padded), BF),
            pltpu.SemaphoreType.DMA((2,)),
            pltpu.SemaphoreType.DMA((tab,)),
        ],
        compiler_params=params(8),
        name="pooled_grad",
    )(*far(weight), grads)


def rep_body(*refs):
    parts, (d_proj, small) = refs[:-2], refs[-2:]
    total = d_proj.shape[0]
    summed = parts[0][...].astype(F32)
    for part in parts[1:]:
        summed = summed + part[...].astype(F32)
    d_proj[...] = summed[:total]
    small[...] = summed[total:].astype(BF)


def rep_sums(parts, total):
    depth, lanes = parts[0].shape
    return pl.pallas_call(
        rep_body,
        out_shape=(
            jax.ShapeDtypeStruct((total, lanes), F32),
            jax.ShapeDtypeStruct((depth - total, lanes), BF),
        ),
        in_specs=[vspec()] * len(parts),
        out_specs=(vspec(), vspec()),
        compiler_params=params(4),
        name="rep_sums",
    )(*parts)


def unpack_body(near, across, d_second, d_in, d_out, d_bil, d_last, arrived, flat):
    tab, _, lanes = arrived.shape
    mine = lax.axis_index("tab")
    for q in range(tab // 2):
        arrived[mine ^ (2 * q)] = near[q]
        arrived[mine ^ (2 * q + 1)] = across[q]
    hidden = d_second.shape[0]
    lines = flat.shape[0] // tab
    for t in range(tab):
        block = arrived[t].astype(F32)
        for i in range(hidden // lanes):
            flat[t * lines : (t + 1) * lines, i * lanes : (i + 1) * lanes] = block[i * lines : (i + 1) * lines]
    d_second[...] = flat[:hidden, :]
    senet, fields = d_in.shape
    width = d_bil.shape[0]
    band = flat[hidden : hidden + senet, :]
    d_in[...] = band[:, :fields]
    d_out[...] = band[:, fields : 2 * fields]
    d_bil[...] = band[:width, 2 * fields : 2 * fields + width]
    column = 2 * fields + width
    pieces = jnp.concatenate([band[:, column + i : column + i + 1] for i in range(hidden // senet)], axis=0)
    row = lax.broadcasted_iota(jnp.int32, (hidden, hidden), 0)
    across = lax.broadcasted_iota(jnp.int32, (hidden, hidden), 1)
    d_last[...] = jnp.sum(jnp.where(row == across, pieces, 0.0), axis=0, keepdims=True)


def unpack(near, across, hidden, senet, fields, width):
    tab = 2 * near.shape[0]
    lines = -(-(hidden + senet) // tab)
    shapes = ((hidden, hidden), (senet, fields), (senet, fields), (width, width), (1, hidden))
    return pl.pallas_call(
        unpack_body,
        out_shape=tuple(jax.ShapeDtypeStruct(s, F32) for s in shapes),
        in_specs=[vspec()] * 2,
        out_specs=tuple(vspec() for _ in shapes),
        scratch_shapes=[pltpu.VMEM((tab,) + near.shape[1:], BF), pltpu.VMEM((lines * tab, hidden), F32)],
        compiler_params=params(4),
        name="unpack",
    )(near, across)


def embeds_order(tab):
    return range(1, tab)


def swap(x, axis, size, bit):
    return lax.ppermute(x, axis, [(i, i ^ bit) for i in range(size)])


def shards(pooled, widths, placement, route, labels, proj, senet_in, senet_out, bilinear, w_first, w_second, w_last):
    tab = lax.axis_size("tab")
    rep = lax.axis_size("rep")
    rep_index = lax.axis_index("rep")
    slots, rep_rows, padded = pooled.shape
    fields, senet = senet_in.shape
    width = proj.shape[2]
    owner = rep_rows // tab
    hidden = w_second.shape[0]
    chips = tab // 2

    weight, *local = embed_slots(widths, placement, pooled, proj.transpose(0, 2, 1), tab)
    arrived = [local[0]] + [swap(local[q], "tab", tab, q) for q in embeds_order(tab)]
    first_turned, second_turned, kron_high, kron_low, back_high, last_column = prepare(
        weight, w_first, w_second, bilinear, w_last.reshape(1, hidden)
    )
    kept, moved, send = owner_pass(
        placement, arrived, labels.reshape(tab, owner), senet_in.T, senet_out, kron_high, kron_low,
        first_turned, second_turned, last_column, w_second, back_high, w_first,
    )
    came = swap(moved, "tab", tab, 1)
    grads = lax.all_to_all(send, "tab", 0, 0, tiled=True)
    parts = first_grad(kept, came, chips, hidden)
    rows = parts[0].shape[0]
    sent = [swap(parts[q], "tab", tab, 2 * q) for q in range(1, chips)]

    base = slots * width
    line = base + hidden // owner * -(-(hidden + senet) // tab)
    summed, scores = proj_grad(widths, placement, pooled, grads, route.reshape(tab, owner), base, line)
    sums = [summed]
    bit = 1
    while bit < rep:
        if len(sums) > 1:
            sums = [sum(part.astype(F32) for part in sums).astype(BF)]
        sums.append(swap(sums[0], "rep", rep, bit))
        bit *= 2
    d_pooled = pooled_grad(pooled, weight, grads)
    d_proj, small = rep_sums(sums, base)
    d_proj = d_proj.reshape(slots, width, padded).transpose(0, 2, 1)
    near = jnp.stack([small] + [swap(small, "tab", tab, 2 * q) for q in range(1, chips)])
    across = swap(near, "tab", tab, 1)
    g_second, g_in, g_out, g_bil, g_last = unpack(near, across, hidden, senet, fields, width)

    first_sum = parts[0].astype(F32)
    for part in sent:
        first_sum = first_sum + part.astype(F32)
    low_bit = rep_index % 2
    halves = first_sum.astype(BF).reshape(2, rows // 2, hidden)
    mine = lax.dynamic_index_in_dim(halves, low_bit, 0, keepdims=False)
    theirs = lax.dynamic_index_in_dim(halves, 1 - low_bit, 0, keepdims=False)
    theirs = swap(theirs, "rep", rep, 1)
    mine = (mine.astype(F32) + theirs.astype(F32)).astype(BF)
    bit = 2
    while bit < rep:
        theirs = swap(mine, "rep", rep, bit)
        mine = (mine.astype(F32) + theirs.astype(F32)).astype(BF)
        bit *= 2
    back = swap(mine, "rep", rep, 1)
    d_first = jnp.where(
        low_bit == 0, jnp.concatenate([mine, back], axis=0), jnp.concatenate([back, mine], axis=0)
    ).astype(F32)
    return (
        scores, d_pooled, d_proj, g_in.T, g_out, g_bil, d_first, g_second, g_last.reshape(hidden),
    )


def solution(mesh):
    placed = (
        P("tab", "rep", None), P(), P(), P("rep", None), P("rep", None),
        P(), P(), P(), P(), P(), P(), P(),
    )
    return jax.shard_map(
        shards,
        mesh=mesh,
        in_specs=placed,
        out_specs=(P("rep", "tab"), P("tab", "rep", None), P("tab", None, None), P(), P(), P(), P("tab", None), P(), P()),
        check_vma=False,
    )
```

profile of v0, /device:TPU:0, one launch (start us, length us, event | category | flops | bytes accessed | tf_op | source)
XLA Modules:
  0.0 79.8 jit_solution(4795243288715211466)
XLA Ops:
  0.7 3.7 %embed_slots.1 = (bf16[256,128]{1,0:T(8,128)(2,1)}, bf16[256,128]{1,0:T(8,128)(2,1)}, bf16[256,128]{1,0:T(8,128)(2,1)}, bf16[256,128]{1,0:T(8,128)(2,1)}, bf16[2...) custom-call(s32[64]{0:T(128)} %widths_hbm.3, ...), custom_call_target="tpu_custom_call" | custom-call | tf_op jit(solution)/shard_map/embed_slots/pallas_call | solution.py:96
  4.9 2.6 %collective-permute-start.1 = (bf16[256,128]{1,0:T(8,128)(2,1)}, bf16[256,128]{1,0:T(8,128)(2,1)S(1)}, u32[]{:S(2)}, u32[]{:S(2)}) collective-permute-start(bf16[256,128]{1,0:T(8,128)(2,1)} %get-tuple-element.42), channel_id=1, source_target_pairs={{0,8},{4,12},{8,0},{12,4},{16,24},{20,28},{24,16},{28,20},{1,9},{5... | collective-permute-start | bytes 196616 | tf_op jit(solution)/shard_map/ppermute | solution.py:573
  7.5 1.8 %collective-permute-start.3 = (bf16[256,128]{1,0:T(8,128)(2,1)}, bf16[256,128]{1,0:T(8,128)(2,1)S(1)}, u32[]{:S(2)}, u32[]{:S(2)}) collective-permute-start(bf16[256,128]{1,0:T(8,128)(2,1)} %get-tuple-element.44), channel_id=1, source_target_pairs={{0,16},{4,20},{8,24},{12,28},{16,0},{20,4},{24,8},{28,12},{1,17},{... | collective-permute-start | bytes 196616 | tf_op jit(solution)/shard_map/ppermute | solution.py:573
  9.3 2.6 %collective-permute-start.5 = (bf16[256,128]{1,0:T(8,128)(2,1)}, bf16[256,128]{1,0:T(8,128)(2,1)S(1)}, u32[]{:S(2)}, u32[]{:S(2)}) collective-permute-start(bf16[256,128]{1,0:T(8,128)(2,1)} %get-tuple-element.46), channel_id=1, source_target_pairs={{0,24},{4,28},{8,16},{12,20},{16,8},{20,12},{24,0},{28,4},{1,25},{... | collective-permute-start | bytes 196616 | tf_op jit(solution)/shard_map/ppermute | solution.py:573
  12.8 3.8 %prepare.1 = (bf16[256,4096]{1,0:T(8,128)(2,1)}, bf16[256,256]{1,0:T(8,128)(2,1)}, bf16[256,256]{1,0:T(8,128)(2,1)}, bf16[256,256]{1,0:T(8,128)(2,1)}, bf16[256,256]{1,0:T(8,128)(2,1)}, /*index=5*/f32[256,1]{1,0:T(8,128)}) custom-call(bf16[256,128]{1,0:T(8,128)(2,1)} %get-tuple-element.48.order.weight_hbm, bf16[4096,256]{1,0:T(8,128)(2,1)} %refs_18_.1, ...), custom_call_target="tpu_custom_call" | custom-call | tf_op jit(solution)/shard_map/prepare/pallas_call | solution.py:163
  17.1 8.5 %owner_pass.1 = (bf16[2304,128]{1,0:T(8,128)(2,1)S(1)}, bf16[2304,128]{1,0:T(8,128)(2,1)S(1)}, bf16[8,336,128]{2,1,0:T(8,128)(2,1)}) custom-call(s32[64]{0:T(128)} %placement_hbm.5, bf16[256,128]{1,0:T(8,128)(2,1)S(1)} %copy-done, bf16[256,128]{1,0:T(8,128)(2,1)S(1)} %collective-permute-done.refs_1_, bf16[256,128]{1,0:T(8,128)(2,1)S(1)} %collective-permute-done.1.refs_2_, ...), custom_call_target="tpu_custom_call" | custom-call | tf_op jit(solution)/shard_map/owner_pass/pallas_call | solution.py:348
  25.6 1.1 %collective-permute-start.13 = (bf16[2304,128]{1,0:T(8,128)(2,1)S(1)}, bf16[2304,128]{1,0:T(8,128)(2,1)S(1)}, u32[]{:S(2)}, u32[]{:S(2)}) collective-permute-start(bf16[2304,128]{1,0:T(8,128)(2,1)S(1)} %get-tuple-element.64), channel_id=1, source_target_pairs={{0,4},{4,0},{8,12},{12,8},{16,20},{20,16},{24,28},{28,24},{1,5},{5... | collective-permute-start | bytes 1769480 | tf_op jit(solution)/shard_map/ppermute | solution.py:573
  26.7 1.6 %collective-permute-done.13.came = bf16[2304,128]{1,0:T(8,128)(2,1)S(1)} collective-permute-done((bf16[2304,128]{1,0:T(8,128)(2,1)S(1)}, bf16[2304,128]{1,0:T(8,128)(2,1)S(1)}, u32[]{:S(2)}, u32[]{:S(2)}) %collective-permute-start.13) | collective-permute-done | bytes 589856 | tf_op jit(solution)/shard_map/ppermute | solution.py:573
  29.2 1.5 %collective-permute-start.15 = (bf16[512,256]{1,0:T(8,128)(2,1)S(1)}, bf16[512,256]{1,0:T(8,128)(2,1)S(1)}, u32[]{:S(2)}, u32[]{:S(2)}) collective-permute-start(bf16[512,256]{1,0:T(8,128)(2,1)S(1)} %get-tuple-element.67), channel_id=1, source_target_pairs={{0,16},{4,20},{8,24},{12,28},{16,0},{20,4},{24,8},{28,12},{1,17},{... | collective-permute-start | bytes 786440 | tf_op jit(solution)/shard_map/ppermute | solution.py:573
  30.7 1.7 %collective-permute-start.16 = (bf16[512,256]{1,0:T(8,128)(2,1)S(1)}, bf16[512,256]{1,0:T(8,128)(2,1)S(1)}, u32[]{:S(2)}, u32[]{:S(2)}) collective-permute-start(bf16[512,256]{1,0:T(8,128)(2,1)S(1)} %get-tuple-element.68), channel_id=1, source_target_pairs={{0,24},{4,28},{8,16},{12,20},{16,8},{20,12},{24,0},{28,4},{1,25},{... | collective-permute-start | bytes 786440 | tf_op jit(solution)/shard_map/ppermute | solution.py:573
  32.4 3.5 %all-to-all-start = ((bf16[8,336,128]{2,1,0:T(8,128)(2,1)}), bf16[8,336,128]{2,1,0:T(8,128)(2,1)S(1)}, u32[]{:S(2)}, u32[]{:S(2)}) async-start(bf16[8,336,128]{2,1,0:T(8,128)(2,1)} %get-tuple-element.55), calls=%async_computation | async-start | bytes 1376256 | tf_op jit(solution)/shard_map/all_to_all | solution.py:597
  36.0 2.1 %collective-permute-done.14 = bf16[512,256]{1,0:T(8,128)(2,1)S(1)} collective-permute-done((bf16[512,256]{1,0:T(8,128)(2,1)S(1)}, bf16[512,256]{1,0:T(8,128)(2,1)S(1)}, u32[]{:S(2)}, u32[]{:S(2)}) %collective-permute-start.14) | collective-permute-done | bytes 262176 | tf_op jit(solution)/shard_map/ppermute | solution.py:573
  38.1 4.7 %collective-permute-done.15 = bf16[512,256]{1,0:T(8,128)(2,1)S(1)} collective-permute-done((bf16[512,256]{1,0:T(8,128)(2,1)S(1)}, bf16[512,256]{1,0:T(8,128)(2,1)S(1)}, u32[]{:S(2)}, u32[]{:S(2)}) %collective-permute-start.15) | collective-permute-done | bytes 262176 | tf_op jit(solution)/shard_map/ppermute | solution.py:573
  43.8 1.6 %collective-permute-start.17 = (bf16[256,256]{1,0:T(8,128)(2,1)S(1)}, bf16[256,256]{1,0:T(8,128)(2,1)S(1)}, u32[]{:S(2)}, u32[]{:S(2)}) collective-permute-start(bf16[256,256]{1,0:T(8,128)(2,1)S(1)} %dynamic-slice_bitcast_fusion), channel_id=1, source_target_pairs={{0,1},{1,0},{2,3},{3,2},{4,5},{5,4},{6,7},{7,6},{8,9},{9,8},{10,11... | collective-permute-start | bytes 393224 | tf_op jit(solution)/shard_map/ppermute | solution.py:573
  45.5 5.1 %all-to-all-done.grads.grads_any = bf16[8,336,128]{2,1,0:T(8,128)(2,1)S(1)} async-done(((bf16[8,336,128]{2,1,0:T(8,128)(2,1)}), bf16[8,336,128]{2,1,0:T(8,128)(2,1)S(1)}, u32[]{:S(2)}, u32[]{:S(2)}) %all-to-all-start) | async-done | bytes 688160 | tf_op jit(solution)/shard_map/all_to_all | solution.py:597
  50.6 3.4 %proj_grad.1 = (bf16[336,128]{1,0:T(8,128)(2,1)S(1)}, f32[1,128]{1,0:T(1,128)}) custom-call(s32[64]{0:T(128)} %widths_hbm.3, s32[64]{0:T(128)} %placement_hbm.5, bf16[8,1024,128]{2,1,0:T(8,128)(2,1)} %pooled.3, bf16[8,336,128]{2,1,0:T(8,128)(2,1)S(1)} %all-to-all-done.grads.grads_any, s32[8,128]{1,0:T(8,128)} %bitcast.28), custom_call_target="tpu_custom_call" | custom-call | tf_op jit(solution)/shard_map/proj_grad/pallas_call | solution.py:434
  53.9 1.6 %collective-permute-start.7 = (bf16[336,128]{1,0:T(8,128)(2,1)S(1)}, bf16[336,128]{1,0:T(8,128)(2,1)S(1)}, u32[]{:S(2)}, u32[]{:S(2)}) collective-permute-start(bf16[336,128]{1,0:T(8,128)(2,1)S(1)} %get-tuple-element.57), channel_id=1, source_target_pairs={{0,1},{1,0},{2,3},{3,2},{4,5},{5,4},{6,7},{7,6},{8,9},{9,8},{10,11... | collective-permute-start | bytes 258056 | tf_op jit(solution)/shard_map/ppermute | solution.py:573
  55.6 2.7 %collective-permute-start.18 = (bf16[256,256]{1,0:T(8,128)(2,1)S(1)}, bf16[256,256]{1,0:T(8,128)(2,1)S(1)}, u32[]{:S(2)}, u32[]{:S(2)}) collective-permute-start(bf16[256,256]{1,0:T(8,128)(2,1)S(1)} %fusion.1), channel_id=1, source_target_pairs={{0,2},{1,3},{2,0},{3,1},{4,6},{5,7},{6,4},{7,5},{8,10},{9,11},{10,... | collective-permute-start | bytes 393224 | tf_op jit(solution)/shard_map/ppermute | solution.py:573
  59.2 2.1 %collective-permute-start.8 = (bf16[336,128]{1,0:T(8,128)(2,1)S(1)}, bf16[336,128]{1,0:T(8,128)(2,1)S(1)}, u32[]{:S(2)}, u32[]{:S(2)}) collective-permute-start(bf16[336,128]{1,0:T(8,128)(2,1)S(1)} %add_convert_fusion.2.refs_0_), channel_id=1, source_target_pairs={{0,2},{1,3},{2,0},{3,1},{4,6},{5,7},{6,4},{7,5},{8,10},{9,11},{10,... | collective-permute-start | bytes 258056 | tf_op jit(solution)/shard_map/ppermute | solution.py:573
  61.4 5.6 %collective-permute-done.8.refs_1_ = bf16[336,128]{1,0:T(8,128)(2,1)S(1)} collective-permute-done((bf16[336,128]{1,0:T(8,128)(2,1)S(1)}, bf16[336,128]{1,0:T(8,128)(2,1)S(1)}, u32[]{:S(2)}, u32[]{:S(2)}) %collective-permute-start.8) | collective-permute-done | bytes 86048 | tf_op jit(solution)/shard_map/ppermute | solution.py:573
  67.7 2.5 %collective-permute-start.9 = (bf16[80,128]{1,0:T(8,128)(2,1)S(1)}, bf16[80,128]{1,0:T(8,128)(2,1)S(1)}, u32[]{:S(2)}, u32[]{:S(2)}) collective-permute-start(bf16[80,128]{1,0:T(8,128)(2,1)S(1)} %get-tuple-element.59), channel_id=1, source_target_pairs={{0,8},{4,12},{8,0},{12,4},{16,24},{20,28},{24,16},{28,20},{1,9},{5... | collective-permute-start | bytes 61448 | tf_op jit(solution)/shard_map/ppermute | solution.py:573
  72.0 2.0 %collective-permute-done.10 = bf16[80,128]{1,0:T(8,128)(2,1)S(1)} collective-permute-done((bf16[80,128]{1,0:T(8,128)(2,1)S(1)}, bf16[80,128]{1,0:T(8,128)(2,1)S(1)}, u32[]{:S(2)}, u32[]{:S(2)}) %collective-permute-start.10) | collective-permute-done | bytes 20512 | tf_op jit(solution)/shard_map/ppermute | solution.py:573
  74.0 1.4 %collective-permute-done.11 = bf16[80,128]{1,0:T(8,128)(2,1)S(1)} collective-permute-done((bf16[80,128]{1,0:T(8,128)(2,1)S(1)}, bf16[80,128]{1,0:T(8,128)(2,1)S(1)}, u32[]{:S(2)}, u32[]{:S(2)}) %collective-permute-start.11) | collective-permute-done | bytes 20512 | tf_op jit(solution)/shard_map/ppermute | solution.py:573
  75.5 2.5 %pooled_grad.1 = bf16[8,1024,128]{2,1,0:T(8,128)(2,1)} custom-call(bf16[256,128]{1,0:T(8,128)(2,1)} %get-tuple-element.48.order.weight_hbm, bf16[8,336,128]{2,1,0:T(8,128)(2,1)S(1)} %all-to-all-done.grads.grads_any), custom_call_target="tpu_custom_call" | custom-call | tf_op jit(solution)/shard_map/pooled_grad/pallas_call | solution.py:484
  (38 shorter events, 9.1 us)
Async XLA Ops:
  0.6 11.6 %copy-start.1 = (bf16[256]{0:T(256)(128)(2,1)S(1)}, bf16[256]{0:T(256)(128)(2,1)}, u32[]{:S(2)}) copy-start(bf16[256]{0:T(256)(128)(2,1)} %param.23) | copy-start | bytes 1540
  4.3 12.7 %copy-start = (bf16[256,128]{1,0:T(8,128)(2,1)S(1)}, bf16[256,128]{1,0:T(8,128)(2,1)}, u32[]{:S(2)}) copy-start(bf16[256,128]{1,0:T(8,128)(2,1)} %get-tuple-element.40.refs_0_) | copy-start | bytes 196612
  4.4 4.9 %collective-permute-start = (bf16[256,128]{1,0:T(8,128)(2,1)}, bf16[256,128]{1,0:T(8,128)(2,1)S(1)}, u32[]{:S(2)}, u32[]{:S(2)}) collective-permute-start(bf16[256,128]{1,0:T(8,128)(2,1)} %get-tuple-element.41), channel_id=1, source_target_pairs={{0,4},{4,0},{8,12},{12,8},{16,20},{20,16},{24,28},{28,24},{1,5},{5... | collective-permute-start | bytes 196616 | tf_op jit(solution)/shard_map/ppermute | solution.py:573
  4.9 7.0 %collective-permute-start.1 = (bf16[256,128]{1,0:T(8,128)(2,1)}, bf16[256,128]{1,0:T(8,128)(2,1)S(1)}, u32[]{:S(2)}, u32[]{:S(2)}) collective-permute-start(bf16[256,128]{1,0:T(8,128)(2,1)} %get-tuple-element.42), channel_id=1, source_target_pairs={{0,8},{4,12},{8,0},{12,4},{16,24},{20,28},{24,16},{28,20},{1,9},{5... | collective-permute-start | bytes 196616 | tf_op jit(solution)/shard_map/ppermute | solution.py:573
  7.5 9.1 %collective-permute-start.2 = (bf16[256,128]{1,0:T(8,128)(2,1)}, bf16[256,128]{1,0:T(8,128)(2,1)S(1)}, u32[]{:S(2)}, u32[]{:S(2)}) collective-permute-start(bf16[256,128]{1,0:T(8,128)(2,1)} %get-tuple-element.43), channel_id=1, source_target_pairs={{0,12},{4,8},{8,4},{12,0},{16,28},{20,24},{24,20},{28,16},{1,13},{... | collective-permute-start | bytes 196616 | tf_op jit(solution)/shard_map/ppermute | solution.py:573
  7.5 9.1 %collective-permute-start.3 = (bf16[256,128]{1,0:T(8,128)(2,1)}, bf16[256,128]{1,0:T(8,128)(2,1)S(1)}, u32[]{:S(2)}, u32[]{:S(2)}) collective-permute-start(bf16[256,128]{1,0:T(8,128)(2,1)} %get-tuple-element.44), channel_id=1, source_target_pairs={{0,16},{4,20},{8,24},{12,28},{16,0},{20,4},{24,8},{28,12},{1,17},{... | collective-permute-start | bytes 196616 | tf_op jit(solution)/shard_map/ppermute | solution.py:573
  9.3 7.3 %collective-permute-start.4 = (bf16[256,128]{1,0:T(8,128)(2,1)}, bf16[256,128]{1,0:T(8,128)(2,1)S(1)}, u32[]{:S(2)}, u32[]{:S(2)}) collective-permute-start(bf16[256,128]{1,0:T(8,128)(2,1)} %get-tuple-element.45), channel_id=1, source_target_pairs={{0,20},{4,16},{8,28},{12,24},{16,4},{20,0},{24,12},{28,8},{1,21},{... | collective-permute-start | bytes 196616 | tf_op jit(solution)/shard_map/ppermute | solution.py:573
  9.3 7.3 %collective-permute-start.5 = (bf16[256,128]{1,0:T(8,128)(2,1)}, bf16[256,128]{1,0:T(8,128)(2,1)S(1)}, u32[]{:S(2)}, u32[]{:S(2)}) collective-permute-start(bf16[256,128]{1,0:T(8,128)(2,1)} %get-tuple-element.46), channel_id=1, source_target_pairs={{0,24},{4,28},{8,16},{12,20},{16,8},{20,12},{24,0},{28,4},{1,25},{... | collective-permute-start | bytes 196616 | tf_op jit(solution)/shard_map/ppermute | solution.py:573
  11.9 5.2 %collective-permute-start.6 = (bf16[256,128]{1,0:T(8,128)(2,1)}, bf16[256,128]{1,0:T(8,128)(2,1)S(1)}, u32[]{:S(2)}, u32[]{:S(2)}) collective-permute-start(bf16[256,128]{1,0:T(8,128)(2,1)} %get-tuple-element.47), channel_id=1, source_target_pairs={{0,28},{4,24},{8,20},{12,16},{16,12},{20,8},{24,4},{28,0},{1,29},{... | collective-permute-start | bytes 196616 | tf_op jit(solution)/shard_map/ppermute | solution.py:573
  25.6 2.8 %collective-permute-start.13 = (bf16[2304,128]{1,0:T(8,128)(2,1)S(1)}, bf16[2304,128]{1,0:T(8,128)(2,1)S(1)}, u32[]{:S(2)}, u32[]{:S(2)}) collective-permute-start(bf16[2304,128]{1,0:T(8,128)(2,1)S(1)} %get-tuple-element.64), channel_id=1, source_target_pairs={{0,4},{4,0},{8,12},{12,8},{16,20},{20,16},{24,28},{28,24},{1,5},{5... | collective-permute-start | bytes 1769480 | tf_op jit(solution)/shard_map/ppermute | solution.py:573
  28.8 9.2 %collective-permute-start.14 = (bf16[512,256]{1,0:T(8,128)(2,1)S(1)}, bf16[512,256]{1,0:T(8,128)(2,1)S(1)}, u32[]{:S(2)}, u32[]{:S(2)}) collective-permute-start(bf16[512,256]{1,0:T(8,128)(2,1)S(1)} %get-tuple-element.66), channel_id=1, source_target_pairs={{0,8},{4,12},{8,0},{12,4},{16,24},{20,28},{24,16},{28,20},{1,9},{5... | collective-permute-start | bytes 786440 | tf_op jit(solution)/shard_map/ppermute | solution.py:573
  29.2 13.6 %collective-permute-start.15 = (bf16[512,256]{1,0:T(8,128)(2,1)S(1)}, bf16[512,256]{1,0:T(8,128)(2,1)S(1)}, u32[]{:S(2)}, u32[]{:S(2)}) collective-permute-start(bf16[512,256]{1,0:T(8,128)(2,1)S(1)} %get-tuple-element.67), channel_id=1, source_target_pairs={{0,16},{4,20},{8,24},{12,28},{16,0},{20,4},{24,8},{28,12},{1,17},{... | collective-permute-start | bytes 786440 | tf_op jit(solution)/shard_map/ppermute | solution.py:573
  30.7 12.9 %collective-permute-start.16 = (bf16[512,256]{1,0:T(8,128)(2,1)S(1)}, bf16[512,256]{1,0:T(8,128)(2,1)S(1)}, u32[]{:S(2)}, u32[]{:S(2)}) collective-permute-start(bf16[512,256]{1,0:T(8,128)(2,1)S(1)} %get-tuple-element.68), channel_id=1, source_target_pairs={{0,24},{4,28},{8,16},{12,20},{16,8},{20,12},{24,0},{28,4},{1,25},{... | collective-permute-start | bytes 786440 | tf_op jit(solution)/shard_map/ppermute | solution.py:573
  32.4 18.2 %all-to-all-start = ((bf16[8,336,128]{2,1,0:T(8,128)(2,1)}), bf16[8,336,128]{2,1,0:T(8,128)(2,1)S(1)}, u32[]{:S(2)}, u32[]{:S(2)}) async-start(bf16[8,336,128]{2,1,0:T(8,128)(2,1)} %get-tuple-element.55), calls=%async_computation | async-start | bytes 1376256 | tf_op jit(solution)/shard_map/all_to_all | solution.py:597
  43.8 11.7 %collective-permute-start.17 = (bf16[256,256]{1,0:T(8,128)(2,1)S(1)}, bf16[256,256]{1,0:T(8,128)(2,1)S(1)}, u32[]{:S(2)}, u32[]{:S(2)}) collective-permute-start(bf16[256,256]{1,0:T(8,128)(2,1)S(1)} %dynamic-slice_bitcast_fusion), channel_id=1, source_target_pairs={{0,1},{1,0},{2,3},{3,2},{4,5},{5,4},{6,7},{7,6},{8,9},{9,8},{10,11... | collective-permute-start | bytes 393224 | tf_op jit(solution)/shard_map/ppermute | solution.py:573
  53.9 5.3 %collective-permute-start.7 = (bf16[336,128]{1,0:T(8,128)(2,1)S(1)}, bf16[336,128]{1,0:T(8,128)(2,1)S(1)}, u32[]{:S(2)}, u32[]{:S(2)}) collective-permute-start(bf16[336,128]{1,0:T(8,128)(2,1)S(1)} %get-tuple-element.57), channel_id=1, source_target_pairs={{0,1},{1,0},{2,3},{3,2},{4,5},{5,4},{6,7},{7,6},{8,9},{9,8},{10,11... | collective-permute-start | bytes 258056 | tf_op jit(solution)/shard_map/ppermute | solution.py:573
  55.6 16.1 %collective-permute-start.18 = (bf16[256,256]{1,0:T(8,128)(2,1)S(1)}, bf16[256,256]{1,0:T(8,128)(2,1)S(1)}, u32[]{:S(2)}, u32[]{:S(2)}) collective-permute-start(bf16[256,256]{1,0:T(8,128)(2,1)S(1)} %fusion.1), channel_id=1, source_target_pairs={{0,2},{1,3},{2,0},{3,1},{4,6},{5,7},{6,4},{7,5},{8,10},{9,11},{10,... | collective-permute-start | bytes 393224 | tf_op jit(solution)/shard_map/ppermute | solution.py:573
  59.2 7.8 %collective-permute-start.8 = (bf16[336,128]{1,0:T(8,128)(2,1)S(1)}, bf16[336,128]{1,0:T(8,128)(2,1)S(1)}, u32[]{:S(2)}, u32[]{:S(2)}) collective-permute-start(bf16[336,128]{1,0:T(8,128)(2,1)S(1)} %add_convert_fusion.2.refs_0_), channel_id=1, source_target_pairs={{0,2},{1,3},{2,0},{3,1},{4,6},{5,7},{6,4},{7,5},{8,10},{9,11},{10,... | collective-permute-start | bytes 258056 | tf_op jit(solution)/shard_map/ppermute | solution.py:573
  67.7 4.3 %collective-permute-start.9 = (bf16[80,128]{1,0:T(8,128)(2,1)S(1)}, bf16[80,128]{1,0:T(8,128)(2,1)S(1)}, u32[]{:S(2)}, u32[]{:S(2)}) collective-permute-start(bf16[80,128]{1,0:T(8,128)(2,1)S(1)} %get-tuple-element.59), channel_id=1, source_target_pairs={{0,8},{4,12},{8,0},{12,4},{16,24},{20,28},{24,16},{28,20},{1,9},{5... | collective-permute-start | bytes 61448 | tf_op jit(solution)/shard_map/ppermute | solution.py:573
  70.2 3.8 %collective-permute-start.10 = (bf16[80,128]{1,0:T(8,128)(2,1)S(1)}, bf16[80,128]{1,0:T(8,128)(2,1)S(1)}, u32[]{:S(2)}, u32[]{:S(2)}) collective-permute-start(bf16[80,128]{1,0:T(8,128)(2,1)S(1)} %get-tuple-element.59), channel_id=1, source_target_pairs={{0,16},{4,20},{8,24},{12,28},{16,0},{20,4},{24,8},{28,12},{1,17},{... | collective-permute-start | bytes 61448 | tf_op jit(solution)/shard_map/ppermute | solution.py:573
  70.7 4.7 %collective-permute-start.11 = (bf16[80,128]{1,0:T(8,128)(2,1)S(1)}, bf16[80,128]{1,0:T(8,128)(2,1)S(1)}, u32[]{:S(2)}, u32[]{:S(2)}) collective-permute-start(bf16[80,128]{1,0:T(8,128)(2,1)S(1)} %get-tuple-element.59), channel_id=1, source_target_pairs={{0,24},{4,28},{8,16},{12,20},{16,8},{20,12},{24,0},{28,4},{1,25},{... | collective-permute-start | bytes 61448 | tf_op jit(solution)/shard_map/ppermute | solution.py:573
  71.7 7.2 %collective-permute-start.19 = (bf16[256,256]{1,0:T(8,128)(2,1)S(1)}, bf16[256,256]{1,0:T(8,128)(2,1)S(1)}, u32[]{:S(2)}, u32[]{:S(2)}) collective-permute-start(bf16[256,256]{1,0:T(8,128)(2,1)S(1)} %add_convert_fusion.1), channel_id=1, source_target_pairs={{0,1},{1,0},{2,3},{3,2},{4,5},{5,4},{6,7},{7,6},{8,9},{9,8},{10,11... | collective-permute-start | bytes 393224 | tf_op jit(solution)/shard_map/ppermute | solution.py:573
  75.4 2.6 %collective-permute-start.12 = (bf16[4,80,128]{2,1,0:T(8,128)(2,1)S(1)}, bf16[4,80,128]{2,1,0:T(8,128)(2,1)S(1)}, u32[]{:S(2)}, u32[]{:S(2)}) collective-permute-start(bf16[4,80,128]{2,1,0:T(8,128)(2,1)S(1)} %pad_maximum_fusion.near), channel_id=1, source_target_pairs={{0,4},{4,0},{8,12},{12,8},{16,20},{20,16},{24,28},{28,24},{1,5},{5... | collective-permute-start | bytes 245768 | tf_op jit(solution)/shard_map/ppermute | solution.py:573
where the time goes:
time: 80.1 us; the launch traced here: 79.8 us
  starting transfers between devices  28.3 us (35%)
  waiting for transfers between devices  25.1 us (31%)
  Pallas kernels  23.8 us (30%)
  other arithmetic  1.14 us (1%)
  between operations  0.83 us (1%)
    ppermute x20, starting transfers between devices, swap(): return lax.ppermute(x, axis, [(i, i ^ bit) for i in range(size)])  24.8 us
    ppermute x20, waiting for transfers between devices, swap(): return lax.ppermute(x, axis, [(i, i ^ bit) for i in range(size)])  20 us
    pallas_call x1, Pallas kernels, owner_pass(): pl.pallas_call(owner_body, out_shape=(pair, pair, pltpu.HBM((tab, depth,...  8.5 us
    all_to_all x1, waiting for transfers between devices, shards(): grads = lax.all_to_all(send, 'tab', 0, 0, tiled=True)  5.09 us
    pallas_call x1, Pallas kernels, prepare(): pl.pallas_call(prepare_body, out_shape=tuple((pltpu.HBM(s, d) for s, d in...  3.75 us
    pallas_call x1, Pallas kernels, embed_slots(): pl.pallas_call(embed_body, out_shape=(pltpu.HBM((slots * width, padded),...  3.69 us
    all_to_all x1, starting transfers between devices, shards(): grads = lax.all_to_all(send, 'tab', 0, 0, tiled=True)  3.54 us
    pallas_call x1, Pallas kernels, proj_grad(): pl.pallas_call(functools.partial(proj_body, line=(total, line)), out_shap...  3.36 us
  transfers between devices with their start and end apart: 21, of which 11 were waited for; matrix products, arithmetic and copies ran while one was open for 1% of the time, Pallas kernels for 14%

commit v1 on v0

--- a/solution.py
+++ b/solution.py
@@ -393,26 +393,26 @@
 
 
 def proj_body(
-    widths_hbm, placement_hbm, pooled, grads, route_hbm, summed_out, scores,
-    widths, placement, rows_in, route, sems, in_sems, *, line,
+    widths_hbm, placement_hbm, pooled, grads_any, route_hbm, summed_out, scores,
+    widths, placement, rows_in, grads, route, sems, in_sems, *, line,
 ):
     slots, _, padded = rows_in.shape
     tab, _, owner = grads.shape
     mine = lax.axis_index("tab")
     first = mine * slots
-    pairs = ((placement_hbm, placement), (widths_hbm, widths), (route_hbm, route))
+    pairs = ((grads_any, grads), (placement_hbm, placement), (widths_hbm, widths), (route_hbm, route))
     copies = [pltpu.make_async_copy(source, target, sems.at[i]) for i, (source, target) in enumerate(pairs)]
     large = [pltpu.make_async_copy(pooled.at[s], rows_in.at[s], in_sems.at[s]) for s in range(slots)]
     for copy in copies + large:
         copy.start()
+    for copy in copies:
+        copy.wait()
     total = line[0]
     width = total // slots
     small = grads[0, total:, :].astype(F32)
     for o in range(1, tab):
         small = small + grads[o, total:, :].astype(F32)
     summed_out[total:, :] = small.astype(BF)
-    for copy in copies:
-        copy.wait()
     wanted = route[pl.ds(mine, 1), :]
     spot = lax.broadcasted_iota(jnp.int32, (owner, owner), 0)
     found = jnp.zeros((2, owner), F32)
@@ -434,14 +434,15 @@
     return pl.pallas_call(
         functools.partial(proj_body, line=(total, line)),
         out_shape=(jax.ShapeDtypeStruct((depth, padded), BF), jax.ShapeDtypeStruct((1, owner), F32)),
-        in_specs=[hspec(), hspec(), hspec(), vspec(), hspec()],
+        in_specs=[hspec()] * 5,
         out_specs=(vspec(), vspec()),
         scratch_shapes=[
             pltpu.SMEM((fields,), jnp.int32),
             pltpu.SMEM((fields,), jnp.int32),
             pltpu.VMEM(pooled.shape, BF),
+            pltpu.VMEM(grads.shape, BF),
             pltpu.VMEM(route.shape, jnp.int32),
-            pltpu.SemaphoreType.DMA((3,)),
+            pltpu.SemaphoreType.DMA((4,)),
             pltpu.SemaphoreType.DMA((slots,)),
         ],
         compiler_params=params(8),
@@ -506,16 +507,18 @@
     for part in parts[1:]:
         summed = summed + part[...].astype(F32)
     d_proj[...] = summed[:total]
-    small[...] = summed[total:].astype(BF)
-
-
-def rep_sums(parts, total):
+    lines = summed[total:].astype(BF)
+    for t in range(small.shape[0]):
+        small[t] = lines
+
+
+def rep_sums(parts, total, tab):
     depth, lanes = parts[0].shape
     return pl.pallas_call(
         rep_body,
         out_shape=(
             jax.ShapeDtypeStruct((total, lanes), F32),
-            jax.ShapeDtypeStruct((depth - total, lanes), BF),
+            jax.ShapeDtypeStruct((tab, depth - total, lanes), BF),
         ),
         in_specs=[vspec()] * len(parts),
         out_specs=(vspec(), vspec()),
@@ -524,12 +527,8 @@
     )(*parts)
 
 
-def unpack_body(near, across, d_second, d_in, d_out, d_bil, d_last, arrived, flat):
+def unpack_body(arrived, d_second, d_in, d_out, d_bil, d_last, flat):
     tab, _, lanes = arrived.shape
-    mine = lax.axis_index("tab")
-    for q in range(tab // 2):
-        arrived[mine ^ (2 * q)] = near[q]
-        arrived[mine ^ (2 * q + 1)] = across[q]
     hidden = d_second.shape[0]
     lines = flat.shape[0] // tab
     for t in range(tab):
@@ -550,19 +549,19 @@
     d_last[...] = jnp.sum(jnp.where(row == across, pieces, 0.0), axis=0, keepdims=True)
 
 
-def unpack(near, across, hidden, senet, fields, width):
-    tab = 2 * near.shape[0]
+def unpack(arrived, hidden, senet, fields, width):
+    tab = arrived.shape[0]
     lines = -(-(hidden + senet) // tab)
     shapes = ((hidden, hidden), (senet, fields), (senet, fields), (width, width), (1, hidden))
     return pl.pallas_call(
         unpack_body,
         out_shape=tuple(jax.ShapeDtypeStruct(s, F32) for s in shapes),
-        in_specs=[vspec()] * 2,
+        in_specs=[vspec()],
         out_specs=tuple(vspec() for _ in shapes),
-        scratch_shapes=[pltpu.VMEM((tab,) + near.shape[1:], BF), pltpu.VMEM((lines * tab, hidden), F32)],
+        scratch_shapes=[pltpu.VMEM((lines * tab, hidden), F32)],
         compiler_params=params(4),
         name="unpack",
-    )(near, across)
+    )(arrived)
 
 
 def embeds_order(tab):
@@ -602,19 +601,12 @@
     base = slots * width
     line = base + hidden // owner * -(-(hidden + senet) // tab)
     summed, scores = proj_grad(widths, placement, pooled, grads, route.reshape(tab, owner), base, line)
-    sums = [summed]
-    bit = 1
-    while bit < rep:
-        if len(sums) > 1:
-            sums = [sum(part.astype(F32) for part in sums).astype(BF)]
-        sums.append(swap(sums[0], "rep", rep, bit))
-        bit *= 2
+    sums = [summed] + [swap(summed, "rep", rep, q) for q in range(1, rep)]
     d_pooled = pooled_grad(pooled, weight, grads)
-    d_proj, small = rep_sums(sums, base)
+    d_proj, small = rep_sums(sums, base, tab)
     d_proj = d_proj.reshape(slots, width, padded).transpose(0, 2, 1)
-    near = jnp.stack([small] + [swap(small, "tab", tab, 2 * q) for q in range(1, chips)])
-    across = swap(near, "tab", tab, 1)
-    g_second, g_in, g_out, g_bil, g_last = unpack(near, across, hidden, senet, fields, width)
+    small = lax.all_to_all(small, "tab", 0, 0, tiled=True)
+    g_second, g_in, g_out, g_bil, g_last = unpack(small, hidden, senet, fields, width)
 
     first_sum = parts[0].astype(F32)
     for part in sent:

time: 80.1 us -> 78 us (0.974)
  waiting for transfers between devices: 25.1 us -> 20.1 us
  starting transfers between devices: 28.3 us -> 30.9 us
    all_to_all x1, waiting for transfers between devices: 5.09 us -> 0.01 us  [shards(): grads = lax.all_to_all(send, 'tab', 0, 0, tiled=True)]
    all_to_all x0 -> x1, starting transfers between devices: none -> 4.48 us  [shards(): small = lax.all_to_all(small, 'tab', 0, 0, tiled=True)]
    ppermute x20 -> x17, starting transfers between devices: 24.8 us -> 22.9 us  [swap(): return lax.ppermute(x, axis, [(i, i ^ bit) for i in range(size)])]
    all_to_all x0 -> x1, waiting for transfers between devices: none -> 1.74 us  [shards(): small = lax.all_to_all(small, 'tab', 0, 0, tiled=True)]
    ppermute x20 -> x17, waiting for transfers between devices: 20 us -> 18.4 us  [swap(): return lax.ppermute(x, axis, [(i, i ^ bit) for i in range(size)])]
  transfers between devices with their start and end apart: 21 -> 19, of which waited for: 11 -> 10; matrix products, arithmetic and copies ran while one was open for 1% -> 1% of each run, Pallas kernels for 14% -> 15%
where the time goes in v1:
time: 78 us; the launch traced here: 77.6 us
  starting transfers between devices  30.9 us (40%)
  Pallas kernels  24.1 us (31%)
  waiting for transfers between devices  20.1 us (26%)
  other arithmetic  1.1 us (1%)
  between operations  0.78 us (1%)
    ppermute x17, starting transfers between devices, swap(): return lax.ppermute(x, axis, [(i, i ^ bit) for i in range(size)])  22.9 us
    ppermute x17, waiting for transfers between devices, swap(): return lax.ppermute(x, axis, [(i, i ^ bit) for i in range(size)])  18.4 us
    pallas_call x1, Pallas kernels, owner_pass(): pl.pallas_call(owner_body, out_shape=(pair, pair, pltpu.HBM((tab, depth,...  8.49 us
    all_to_all x1, starting transfers between devices, shards(): small = lax.all_to_all(small, 'tab', 0, 0, tiled=True)  4.48 us
    pallas_call x1, Pallas kernels, prepare(): pl.pallas_call(prepare_body, out_shape=tuple((pltpu.HBM(s, d) for s, d in...  3.75 us
    pallas_call x1, Pallas kernels, embed_slots(): pl.pallas_call(embed_body, out_shape=(pltpu.HBM((slots * width, padded),...  3.68 us
    pallas_call x1, Pallas kernels, proj_grad(): pl.pallas_call(functools.partial(proj_body, line=(total, line)), out_shap...  3.65 us
    all_to_all x1, starting transfers between devices, shards(): grads = lax.all_to_all(send, 'tab', 0, 0, tiled=True)  3.54 us
  transfers between devices with their start and end apart: 19, of which 10 were waited for; matrix products, arithmetic and copies ran while one was open for 1% of the time, Pallas kernels for 15%

profile of v1, /device:TPU:0, one launch (start us, length us, event | category | flops | bytes accessed | tf_op | source)
XLA Modules:
  0.0 77.6 jit_solution(1851816619359308593)
XLA Ops:
  0.7 3.7 %embed_slots.1 = (bf16[256,128]{1,0:T(8,128)(2,1)}, bf16[256,128]{1,0:T(8,128)(2,1)}, bf16[256,128]{1,0:T(8,128)(2,1)}, bf16[256,128]{1,0:T(8,128)(2,1)}, bf16[2...) custom-call(s32[64]{0:T(128)} %widths_hbm.3, ...), custom_call_target="tpu_custom_call" | custom-call | tf_op jit(solution)/shard_map/embed_slots/pallas_call | solution.py:96
  4.9 2.6 %collective-permute-start.1 = (bf16[256,128]{1,0:T(8,128)(2,1)}, bf16[256,128]{1,0:T(8,128)(2,1)S(1)}, u32[]{:S(2)}, u32[]{:S(2)}) collective-permute-start(bf16[256,128]{1,0:T(8,128)(2,1)} %get-tuple-element.42), channel_id=1, source_target_pairs={{0,8},{4,12},{8,0},{12,4},{16,24},{20,28},{24,16},{28,20},{1,9},{5... | collective-permute-start | bytes 196616 | tf_op jit(solution)/shard_map/ppermute | solution.py:572
  7.5 1.8 %collective-permute-start.3 = (bf16[256,128]{1,0:T(8,128)(2,1)}, bf16[256,128]{1,0:T(8,128)(2,1)S(1)}, u32[]{:S(2)}, u32[]{:S(2)}) collective-permute-start(bf16[256,128]{1,0:T(8,128)(2,1)} %get-tuple-element.44), channel_id=1, source_target_pairs={{0,16},{4,20},{8,24},{12,28},{16,0},{20,4},{24,8},{28,12},{1,17},{... | collective-permute-start | bytes 196616 | tf_op jit(solution)/shard_map/ppermute | solution.py:572
  9.3 2.6 %collective-permute-start.5 = (bf16[256,128]{1,0:T(8,128)(2,1)}, bf16[256,128]{1,0:T(8,128)(2,1)S(1)}, u32[]{:S(2)}, u32[]{:S(2)}) collective-permute-start(bf16[256,128]{1,0:T(8,128)(2,1)} %get-tuple-element.46), channel_id=1, source_target_pairs={{0,24},{4,28},{8,16},{12,20},{16,8},{20,12},{24,0},{28,4},{1,25},{... | collective-permute-start | bytes 196616 | tf_op jit(solution)/shard_map/ppermute | solution.py:572
  12.8 3.8 %prepare.1 = (bf16[256,4096]{1,0:T(8,128)(2,1)}, bf16[256,256]{1,0:T(8,128)(2,1)}, bf16[256,256]{1,0:T(8,128)(2,1)}, bf16[256,256]{1,0:T(8,128)(2,1)}, bf16[256,256]{1,0:T(8,128)(2,1)}, /*index=5*/f32[256,1]{1,0:T(8,128)}) custom-call(bf16[256,128]{1,0:T(8,128)(2,1)} %get-tuple-element.48.order.weight_hbm, bf16[4096,256]{1,0:T(8,128)(2,1)} %refs_18_.1, ...), custom_call_target="tpu_custom_call" | custom-call | tf_op jit(solution)/shard_map/prepare/pallas_call | solution.py:163
  17.1 8.5 %owner_pass.1 = (bf16[2304,128]{1,0:T(8,128)(2,1)S(1)}, bf16[2304,128]{1,0:T(8,128)(2,1)S(1)}, bf16[8,336,128]{2,1,0:T(8,128)(2,1)}) custom-call(s32[64]{0:T(128)} %placement_hbm.5, bf16[256,128]{1,0:T(8,128)(2,1)S(1)} %copy-done, bf16[256,128]{1,0:T(8,128)(2,1)S(1)} %collective-permute-done.refs_1_, bf16[256,128]{1,0:T(8,128)(2,1)S(1)} %collective-permute-done.1.refs_2_, ...), custom_call_target="tpu_custom_call" | custom-call | tf_op jit(solution)/shard_map/owner_pass/pallas_call | solution.py:348
  26.7 1.6 %collective-permute-done.10.came = bf16[2304,128]{1,0:T(8,128)(2,1)S(1)} collective-permute-done((bf16[2304,128]{1,0:T(8,128)(2,1)S(1)}, bf16[2304,128]{1,0:T(8,128)(2,1)S(1)}, u32[]{:S(2)}, u32[]{:S(2)}) %collective-permute-start.10) | collective-permute-done | bytes 589856 | tf_op jit(solution)/shard_map/ppermute | solution.py:572
  29.2 1.5 %collective-permute-start.12 = (bf16[512,256]{1,0:T(8,128)(2,1)S(1)}, bf16[512,256]{1,0:T(8,128)(2,1)S(1)}, u32[]{:S(2)}, u32[]{:S(2)}) collective-permute-start(bf16[512,256]{1,0:T(8,128)(2,1)S(1)} %get-tuple-element.67), channel_id=1, source_target_pairs={{0,16},{4,20},{8,24},{12,28},{16,0},{20,4},{24,8},{28,12},{1,17},{... | collective-permute-start | bytes 786440 | tf_op jit(solution)/shard_map/ppermute | solution.py:572
  30.7 1.7 %collective-permute-start.13 = (bf16[512,256]{1,0:T(8,128)(2,1)S(1)}, bf16[512,256]{1,0:T(8,128)(2,1)S(1)}, u32[]{:S(2)}, u32[]{:S(2)}) collective-permute-start(bf16[512,256]{1,0:T(8,128)(2,1)S(1)} %get-tuple-element.68), channel_id=1, source_target_pairs={{0,24},{4,28},{8,16},{12,20},{16,8},{20,12},{24,0},{28,4},{1,25},{... | collective-permute-start | bytes 786440 | tf_op jit(solution)/shard_map/ppermute | solution.py:572
  32.4 3.5 %all-to-all-start = ((bf16[8,336,128]{2,1,0:T(8,128)(2,1)}), bf16[8,336,128]{2,1,0:T(8,128)(2,1)S(1)}, u32[]{:S(2)}, u32[]{:S(2)}) async-start(bf16[8,336,128]{2,1,0:T(8,128)(2,1)} %get-tuple-element.55), calls=%async_computation | async-start | bytes 1376256 | tf_op jit(solution)/shard_map/all_to_all | solution.py:596
  35.9 2.1 %collective-permute-done.11 = bf16[512,256]{1,0:T(8,128)(2,1)S(1)} collective-permute-done((bf16[512,256]{1,0:T(8,128)(2,1)S(1)}, bf16[512,256]{1,0:T(8,128)(2,1)S(1)}, u32[]{:S(2)}, u32[]{:S(2)}) %collective-permute-start.11) | collective-permute-done | bytes 262176 | tf_op jit(solution)/shard_map/ppermute | solution.py:572
  38.0 4.7 %collective-permute-done.12 = bf16[512,256]{1,0:T(8,128)(2,1)S(1)} collective-permute-done((bf16[512,256]{1,0:T(8,128)(2,1)S(1)}, bf16[512,256]{1,0:T(8,128)(2,1)S(1)}, u32[]{:S(2)}, u32[]{:S(2)}) %collective-permute-start.12) | collective-permute-done | bytes 262176 | tf_op jit(solution)/shard_map/ppermute | solution.py:572
  43.8 1.7 %collective-permute-start.14 = (bf16[256,256]{1,0:T(8,128)(2,1)S(1)}, bf16[256,256]{1,0:T(8,128)(2,1)S(1)}, u32[]{:S(2)}, u32[]{:S(2)}) collective-permute-start(bf16[256,256]{1,0:T(8,128)(2,1)S(1)} %dynamic-slice_bitcast_fusion), channel_id=1, source_target_pairs={{0,1},{1,0},{2,3},{3,2},{4,5},{5,4},{6,7},{7,6},{8,9},{9,8},{10,11... | collective-permute-start | bytes 393224 | tf_op jit(solution)/shard_map/ppermute | solution.py:572
  45.5 3.4 %collective-permute-done.14 = bf16[256,256]{1,0:T(8,128)(2,1)S(1)} collective-permute-done((bf16[256,256]{1,0:T(8,128)(2,1)S(1)}, bf16[256,256]{1,0:T(8,128)(2,1)S(1)}, u32[]{:S(2)}, u32[]{:S(2)}) %collective-permute-start.14) | collective-permute-done | bytes 131104 | tf_op jit(solution)/shard_map/ppermute | solution.py:572
  48.9 2.6 %collective-permute-start.15 = (bf16[256,256]{1,0:T(8,128)(2,1)S(1)}, bf16[256,256]{1,0:T(8,128)(2,1)S(1)}, u32[]{:S(2)}, u32[]{:S(2)}) collective-permute-start(bf16[256,256]{1,0:T(8,128)(2,1)S(1)} %fusion.1), channel_id=1, source_target_pairs={{0,2},{1,3},{2,0},{3,1},{4,6},{5,7},{6,4},{7,5},{8,10},{9,11},{10,... | collective-permute-start | bytes 393224 | tf_op jit(solution)/shard_map/ppermute | solution.py:572
  51.6 3.6 %proj_grad.1 = (bf16[336,128]{1,0:T(8,128)(2,1)S(1)}, f32[1,128]{1,0:T(1,128)}) custom-call(s32[64]{0:T(128)} %widths_hbm.3, s32[64]{0:T(128)} %placement_hbm.5, bf16[8,1024,128]{2,1,0:T(8,128)(2,1)} %pooled.3, bf16[8,336,128]{2,1,0:T(8,128)(2,1)S(1)} %all-to-all-done.grads_any, s32[8,128]{1,0:T(8,128)} %bitcast.20), custom_call_target="tpu_custom_call" | custom-call | tf_op jit(solution)/shard_map/proj_grad/pallas_call | solution.py:434
  55.2 1.6 %collective-permute-start.7 = (bf16[336,128]{1,0:T(8,128)(2,1)S(1)}, bf16[336,128]{1,0:T(8,128)(2,1)S(1)}, u32[]{:S(2)}, u32[]{:S(2)}) collective-permute-start(bf16[336,128]{1,0:T(8,128)(2,1)S(1)} %get-tuple-element.57.refs_0_), channel_id=1, source_target_pairs={{0,1},{1,0},{2,3},{3,2},{4,5},{5,4},{6,7},{7,6},{8,9},{9,8},{10,11... | collective-permute-start | bytes 258056 | tf_op jit(solution)/shard_map/ppermute | solution.py:572
  56.9 1.6 %collective-permute-start.8 = (bf16[336,128]{1,0:T(8,128)(2,1)S(1)}, bf16[336,128]{1,0:T(8,128)(2,1)S(1)}, u32[]{:S(2)}, u32[]{:S(2)}) collective-permute-start(bf16[336,128]{1,0:T(8,128)(2,1)S(1)} %get-tuple-element.57.refs_0_), channel_id=1, source_target_pairs={{0,2},{1,3},{2,0},{3,1},{4,6},{5,7},{6,4},{7,5},{8,10},{9,11},{10,... | collective-permute-start | bytes 258056 | tf_op jit(solution)/shard_map/ppermute | solution.py:572
  58.4 1.2 %collective-permute-start.9 = (bf16[336,128]{1,0:T(8,128)(2,1)S(1)}, bf16[336,128]{1,0:T(8,128)(2,1)S(1)}, u32[]{:S(2)}, u32[]{:S(2)}) collective-permute-start(bf16[336,128]{1,0:T(8,128)(2,1)S(1)} %get-tuple-element.57.refs_0_), channel_id=1, source_target_pairs={{0,3},{1,2},{2,1},{3,0},{4,7},{5,6},{6,5},{7,4},{8,11},{9,10},{10,... | collective-permute-start | bytes 258056 | tf_op jit(solution)/shard_map/ppermute | solution.py:572
  59.9 4.0 %collective-permute-done.8.refs_2_ = bf16[336,128]{1,0:T(8,128)(2,1)S(1)} collective-permute-done((bf16[336,128]{1,0:T(8,128)(2,1)S(1)}, bf16[336,128]{1,0:T(8,128)(2,1)S(1)}, u32[]{:S(2)}, u32[]{:S(2)}) %collective-permute-start.8) | collective-permute-done | bytes 86048 | tf_op jit(solution)/shard_map/ppermute | solution.py:572
  65.5 4.5 %all-to-all-start.1 = ((bf16[8,80,128]{2,1,0:T(8,128)(2,1)}), bf16[8,80,128]{2,1,0:T(8,128)(2,1)S(1)}, u32[]{:S(2)}, u32[]{:S(2)}) async-start(bf16[8,80,128]{2,1,0:T(8,128)(2,1)} %get-tuple-element.59), calls=%async_computation.1 | async-start | bytes 327680 | tf_op jit(solution)/shard_map/all_to_all | solution.py:608
  70.1 1.5 %collective-permute-start.16 = (bf16[256,256]{1,0:T(8,128)(2,1)S(1)}, bf16[256,256]{1,0:T(8,128)(2,1)S(1)}, u32[]{:S(2)}, u32[]{:S(2)}) collective-permute-start(bf16[256,256]{1,0:T(8,128)(2,1)S(1)} %add_convert_fusion.1), channel_id=1, source_target_pairs={{0,1},{1,0},{2,3},{3,2},{4,5},{5,4},{6,7},{7,6},{8,9},{9,8},{10,11... | collective-permute-start | bytes 393224 | tf_op jit(solution)/shard_map/ppermute | solution.py:572
  71.6 2.5 %pooled_grad.1 = bf16[8,1024,128]{2,1,0:T(8,128)(2,1)} custom-call(bf16[256,128]{1,0:T(8,128)(2,1)} %get-tuple-element.48.order.weight_hbm, bf16[8,336,128]{2,1,0:T(8,128)(2,1)S(1)} %all-to-all-done.grads_any), custom_call_target="tpu_custom_call" | custom-call | tf_op jit(solution)/shard_map/pooled_grad/pallas_call | solution.py:485
  74.1 1.7 %all-to-all-done.1.arrived = bf16[8,80,128]{2,1,0:T(8,128)(2,1)S(1)} async-done(((bf16[8,80,128]{2,1,0:T(8,128)(2,1)}), bf16[8,80,128]{2,1,0:T(8,128)(2,1)S(1)}, u32[]{:S(2)}, u32[]{:S(2)}) %all-to-all-start.1) | async-done | bytes 163872 | tf_op jit(solution)/shard_map/all_to_all | solution.py:608
  (32 shorter events, 8.7 us)
Async XLA Ops:
  0.6 11.6 %copy-start.1 = (bf16[256]{0:T(256)(128)(2,1)S(1)}, bf16[256]{0:T(256)(128)(2,1)}, u32[]{:S(2)}) copy-start(bf16[256]{0:T(256)(128)(2,1)} %param.23) | copy-start | bytes 1540
  4.3 12.7 %copy-start = (bf16[256,128]{1,0:T(8,128)(2,1)S(1)}, bf16[256,128]{1,0:T(8,128)(2,1)}, u32[]{:S(2)}) copy-start(bf16[256,128]{1,0:T(8,128)(2,1)} %get-tuple-element.40.refs_0_) | copy-start | bytes 196612
  4.4 4.9 %collective-permute-start = (bf16[256,128]{1,0:T(8,128)(2,1)}, bf16[256,128]{1,0:T(8,128)(2,1)S(1)}, u32[]{:S(2)}, u32[]{:S(2)}) collective-permute-start(bf16[256,128]{1,0:T(8,128)(2,1)} %get-tuple-element.41), channel_id=1, source_target_pairs={{0,4},{4,0},{8,12},{12,8},{16,20},{20,16},{24,28},{28,24},{1,5},{5... | collective-permute-start | bytes 196616 | tf_op jit(solution)/shard_map/ppermute | solution.py:572
  4.9 7.0 %collective-permute-start.1 = (bf16[256,128]{1,0:T(8,128)(2,1)}, bf16[256,128]{1,0:T(8,128)(2,1)S(1)}, u32[]{:S(2)}, u32[]{:S(2)}) collective-permute-start(bf16[256,128]{1,0:T(8,128)(2,1)} %get-tuple-element.42), channel_id=1, source_target_pairs={{0,8},{4,12},{8,0},{12,4},{16,24},{20,28},{24,16},{28,20},{1,9},{5... | collective-permute-start | bytes 196616 | tf_op jit(solution)/shard_map/ppermute | solution.py:572
  7.5 9.1 %collective-permute-start.2 = (bf16[256,128]{1,0:T(8,128)(2,1)}, bf16[256,128]{1,0:T(8,128)(2,1)S(1)}, u32[]{:S(2)}, u32[]{:S(2)}) collective-permute-start(bf16[256,128]{1,0:T(8,128)(2,1)} %get-tuple-element.43), channel_id=1, source_target_pairs={{0,12},{4,8},{8,4},{12,0},{16,28},{20,24},{24,20},{28,16},{1,13},{... | collective-permute-start | bytes 196616 | tf_op jit(solution)/shard_map/ppermute | solution.py:572
  7.5 9.1 %collective-permute-start.3 = (bf16[256,128]{1,0:T(8,128)(2,1)}, bf16[256,128]{1,0:T(8,128)(2,1)S(1)}, u32[]{:S(2)}, u32[]{:S(2)}) collective-permute-start(bf16[256,128]{1,0:T(8,128)(2,1)} %get-tuple-element.44), channel_id=1, source_target_pairs={{0,16},{4,20},{8,24},{12,28},{16,0},{20,4},{24,8},{28,12},{1,17},{... | collective-permute-start | bytes 196616 | tf_op jit(solution)/shard_map/ppermute | solution.py:572
  9.3 7.3 %collective-permute-start.4 = (bf16[256,128]{1,0:T(8,128)(2,1)}, bf16[256,128]{1,0:T(8,128)(2,1)S(1)}, u32[]{:S(2)}, u32[]{:S(2)}) collective-permute-start(bf16[256,128]{1,0:T(8,128)(2,1)} %get-tuple-element.45), channel_id=1, source_target_pairs={{0,20},{4,16},{8,28},{12,24},{16,4},{20,0},{24,12},{28,8},{1,21},{... | collective-permute-start | bytes 196616 | tf_op jit(solution)/shard_map/ppermute | solution.py:572
  9.3 7.3 %collective-permute-start.5 = (bf16[256,128]{1,0:T(8,128)(2,1)}, bf16[256,128]{1,0:T(8,128)(2,1)S(1)}, u32[]{:S(2)}, u32[]{:S(2)}) collective-permute-start(bf16[256,128]{1,0:T(8,128)(2,1)} %get-tuple-element.46), channel_id=1, source_target_pairs={{0,24},{4,28},{8,16},{12,20},{16,8},{20,12},{24,0},{28,4},{1,25},{... | collective-permute-start | bytes 196616 | tf_op jit(solution)/shard_map/ppermute | solution.py:572
  11.9 5.2 %collective-permute-start.6 = (bf16[256,128]{1,0:T(8,128)(2,1)}, bf16[256,128]{1,0:T(8,128)(2,1)S(1)}, u32[]{:S(2)}, u32[]{:S(2)}) collective-permute-start(bf16[256,128]{1,0:T(8,128)(2,1)} %get-tuple-element.47), channel_id=1, source_target_pairs={{0,28},{4,24},{8,20},{12,16},{16,12},{20,8},{24,4},{28,0},{1,29},{... | collective-permute-start | bytes 196616 | tf_op jit(solution)/shard_map/ppermute | solution.py:572
  25.6 2.7 %collective-permute-start.10 = (bf16[2304,128]{1,0:T(8,128)(2,1)S(1)}, bf16[2304,128]{1,0:T(8,128)(2,1)S(1)}, u32[]{:S(2)}, u32[]{:S(2)}) collective-permute-start(bf16[2304,128]{1,0:T(8,128)(2,1)S(1)} %get-tuple-element.64), channel_id=1, source_target_pairs={{0,4},{4,0},{8,12},{12,8},{16,20},{20,16},{24,28},{28,24},{1,5},{5... | collective-permute-start | bytes 1769480 | tf_op jit(solution)/shard_map/ppermute | solution.py:572
  28.8 9.2 %collective-permute-start.11 = (bf16[512,256]{1,0:T(8,128)(2,1)S(1)}, bf16[512,256]{1,0:T(8,128)(2,1)S(1)}, u32[]{:S(2)}, u32[]{:S(2)}) collective-permute-start(bf16[512,256]{1,0:T(8,128)(2,1)S(1)} %get-tuple-element.66), channel_id=1, source_target_pairs={{0,8},{4,12},{8,0},{12,4},{16,24},{20,28},{24,16},{28,20},{1,9},{5... | collective-permute-start | bytes 786440 | tf_op jit(solution)/shard_map/ppermute | solution.py:572
  29.2 13.5 %collective-permute-start.12 = (bf16[512,256]{1,0:T(8,128)(2,1)S(1)}, bf16[512,256]{1,0:T(8,128)(2,1)S(1)}, u32[]{:S(2)}, u32[]{:S(2)}) collective-permute-start(bf16[512,256]{1,0:T(8,128)(2,1)S(1)} %get-tuple-element.67), channel_id=1, source_target_pairs={{0,16},{4,20},{8,24},{12,28},{16,0},{20,4},{24,8},{28,12},{1,17},{... | collective-permute-start | bytes 786440 | tf_op jit(solution)/shard_map/ppermute | solution.py:572
  30.7 13.0 %collective-permute-start.13 = (bf16[512,256]{1,0:T(8,128)(2,1)S(1)}, bf16[512,256]{1,0:T(8,128)(2,1)S(1)}, u32[]{:S(2)}, u32[]{:S(2)}) collective-permute-start(bf16[512,256]{1,0:T(8,128)(2,1)S(1)} %get-tuple-element.68), channel_id=1, source_target_pairs={{0,24},{4,28},{8,16},{12,20},{16,8},{20,12},{24,0},{28,4},{1,25},{... | collective-permute-start | bytes 786440 | tf_op jit(solution)/shard_map/ppermute | solution.py:572
  32.4 19.2 %all-to-all-start = ((bf16[8,336,128]{2,1,0:T(8,128)(2,1)}), bf16[8,336,128]{2,1,0:T(8,128)(2,1)S(1)}, u32[]{:S(2)}, u32[]{:S(2)}) async-start(bf16[8,336,128]{2,1,0:T(8,128)(2,1)} %get-tuple-element.55), calls=%async_computation | async-start | bytes 1376256 | tf_op jit(solution)/shard_map/all_to_all | solution.py:596
  43.8 5.0 %collective-permute-start.14 = (bf16[256,256]{1,0:T(8,128)(2,1)S(1)}, bf16[256,256]{1,0:T(8,128)(2,1)S(1)}, u32[]{:S(2)}, u32[]{:S(2)}) collective-permute-start(bf16[256,256]{1,0:T(8,128)(2,1)S(1)} %dynamic-slice_bitcast_fusion), channel_id=1, source_target_pairs={{0,1},{1,0},{2,3},{3,2},{4,5},{5,4},{6,7},{7,6},{8,9},{9,8},{10,11... | collective-permute-start | bytes 393224 | tf_op jit(solution)/shard_map/ppermute | solution.py:572
  48.9 21.1 %collective-permute-start.15 = (bf16[256,256]{1,0:T(8,128)(2,1)S(1)}, bf16[256,256]{1,0:T(8,128)(2,1)S(1)}, u32[]{:S(2)}, u32[]{:S(2)}) collective-permute-start(bf16[256,256]{1,0:T(8,128)(2,1)S(1)} %fusion.1), channel_id=1, source_target_pairs={{0,2},{1,3},{2,0},{3,1},{4,6},{5,7},{6,4},{7,5},{8,10},{9,11},{10,... | collective-permute-start | bytes 393224 | tf_op jit(solution)/shard_map/ppermute | solution.py:572
  55.2 4.6 %collective-permute-start.7 = (bf16[336,128]{1,0:T(8,128)(2,1)S(1)}, bf16[336,128]{1,0:T(8,128)(2,1)S(1)}, u32[]{:S(2)}, u32[]{:S(2)}) collective-permute-start(bf16[336,128]{1,0:T(8,128)(2,1)S(1)} %get-tuple-element.57.refs_0_), channel_id=1, source_target_pairs={{0,1},{1,0},{2,3},{3,2},{4,5},{5,4},{6,7},{7,6},{8,9},{9,8},{10,11... | collective-permute-start | bytes 258056 | tf_op jit(solution)/shard_map/ppermute | solution.py:572
  56.9 7.0 %collective-permute-start.8 = (bf16[336,128]{1,0:T(8,128)(2,1)S(1)}, bf16[336,128]{1,0:T(8,128)(2,1)S(1)}, u32[]{:S(2)}, u32[]{:S(2)}) collective-permute-start(bf16[336,128]{1,0:T(8,128)(2,1)S(1)} %get-tuple-element.57.refs_0_), channel_id=1, source_target_pairs={{0,2},{1,3},{2,0},{3,1},{4,6},{5,7},{6,4},{7,5},{8,10},{9,11},{10,... | collective-permute-start | bytes 258056 | tf_op jit(solution)/shard_map/ppermute | solution.py:572
  58.4 6.4 %collective-permute-start.9 = (bf16[336,128]{1,0:T(8,128)(2,1)S(1)}, bf16[336,128]{1,0:T(8,128)(2,1)S(1)}, u32[]{:S(2)}, u32[]{:S(2)}) collective-permute-start(bf16[336,128]{1,0:T(8,128)(2,1)S(1)} %get-tuple-element.57.refs_0_), channel_id=1, source_target_pairs={{0,3},{1,2},{2,1},{3,0},{4,7},{5,6},{6,5},{7,4},{8,11},{9,10},{10,... | collective-permute-start | bytes 258056 | tf_op jit(solution)/shard_map/ppermute | solution.py:572
  65.5 10.3 %all-to-all-start.1 = ((bf16[8,80,128]{2,1,0:T(8,128)(2,1)}), bf16[8,80,128]{2,1,0:T(8,128)(2,1)S(1)}, u32[]{:S(2)}, u32[]{:S(2)}) async-start(bf16[8,80,128]{2,1,0:T(8,128)(2,1)} %get-tuple-element.59), calls=%async_computation.1 | async-start | bytes 327680 | tf_op jit(solution)/shard_map/all_to_all | solution.py:608
  70.1 6.6 %collective-permute-start.16 = (bf16[256,256]{1,0:T(8,128)(2,1)S(1)}, bf16[256,256]{1,0:T(8,128)(2,1)S(1)}, u32[]{:S(2)}, u32[]{:S(2)}) collective-permute-start(bf16[256,256]{1,0:T(8,128)(2,1)S(1)} %add_convert_fusion.1), channel_id=1, source_target_pairs={{0,1},{1,0},{2,3},{3,2},{4,5},{5,4},{6,7},{7,6},{8,9},{9,8},{10,11... | collective-permute-start | bytes 393224 | tf_op jit(solution)/shard_map/ppermute | solution.py:572
